TPU v7x, 32 devices: a whole 2x2x4 slice. The times are simulated.
32 devices in a mesh: row: 8 (over y, x, core), col: 4 (over z).
Axes of the slice: x: 2, y: 2, z: 4, core: 2. Of those that a mesh axis runs over, the one named last changes fastest.
Arguments:
- matrix: float32 [16384, 8192], P('row', 'col'), may hold values from -40 to 40
Outputs:
- upper: float32 [256, 8192], P('row', 'col')
- reduced: float32 [16384, 8192], P('row', 'col')
All inputs are finite; a program needn't handle non-finite values.
Results may differ from a plain program's by a relative error of at most 0.0003.
Values sent between devices are 32-bit elements; how exact they have to be, the bound alone decides.
A program may use at most 128 MiB of HBM per device.

v0:
```python
import jax
import jax.numpy as jnp
from jax import lax
from jax.sharding import PartitionSpec as P

PANEL = 256
precise = lax.Precision.HIGHEST


def broadcast(shard, axis, root):
    mine = lax.axis_index(axis) == root
    return lax.psum(jnp.where(mine, shard, jnp.zeros_like(shard)), axis)


def multiply(left, right):
    return jnp.dot(left, right, precision=precise, preferred_element_type=jnp.float32)


def cholesky_pass(block):
    gram = multiply(block.T, block)
    lower = jnp.linalg.cholesky(gram)
    basis = jax.scipy.linalg.solve_triangular(lower, block.T, lower=True).T
    return (basis, lower.T)


def factorize(block):
    first_basis, first_upper = cholesky_pass(block)
    second_basis, second_upper = cholesky_pass(first_basis)
    return (second_basis, multiply(second_upper, first_upper))


def shards(matrix):
    row_count = lax.axis_size("row")
    total_rows = matrix.shape[0] * row_count
    share_rows = PANEL // row_count
    panel = matrix[:, :PANEL]
    local_basis, local_upper = factorize(panel)
    total_gram = lax.psum(multiply(local_upper.T, local_upper), "row")
    whole_upper = jnp.linalg.cholesky(total_gram).T
    change = jax.scipy.linalg.solve_triangular(whole_upper.T, local_upper.T, lower=True).T
    basis = multiply(local_basis, change)
    basis = broadcast(basis, "col", 0)
    full_upper = lax.psum(multiply(basis.T, matrix), "row")
    my_share = lax.dynamic_slice_in_dim(
        full_upper, lax.axis_index("row") * share_rows, share_rows, 0
    )
    projected = matrix - multiply(basis, full_upper)
    scale = jnp.sqrt(jnp.float32(total_rows))
    placed = jnp.concatenate([basis * scale, projected[:, PANEL:]], axis=1)
    reduced = jnp.where(lax.axis_index("col") == 0, placed, projected)
    return (my_share, reduced)


def solution(mesh):
    return jax.shard_map(
        shards,
        mesh=mesh,
        in_specs=(P("row", "col"),),
        out_specs=(P("row", "col"), P("row", "col")),
        check_vma=False,
    )
```

profile of v0, /device:TPU:8, one launch (start us, length us, event | category | flops | bytes accessed | tf_op | source)
XLA Modules:
  0.0 487.8 jit_solution(14583731544222165822)
XLA Ops:
  7.2 5.7 %fusion.7 = f32[256,256]{1,0:T(8,128)S(1)} fusion(f32[2048,2048]{1,0:T(8,128)} %param.4), kind=kOutput, calls=%fused_computation.19 | convolution fusion | flops 1610612736 | bytes 2359296 | tf_op jit(solution)/shard_map/dot_general | solution.py:16
  12.9 3.0 slice_bitcast_fusion
  16.2 11.7 %cholesky.172 = f32[128,128]{1,0:T(8,128)S(1)} custom-call(f32[128,128]{1,0:T(8,128)S(1)} %cholesky.270), custom_call_target="Cholesky" | custom-call | tf_op jit(solution)/shard_map/jit(cholesky)/cholesky | solution.py:21
  27.9 9.8 %custom-call.19 = f32[1,128,128]{1,2,0:T(8,128)S(1)} custom-call(f32[1,128,128]{2,1,0:T(8,128)S(1)} %get-tuple-element.71), custom_call_target="InvertDiagBlocksLowerTriangular" | custom-call | tf_op jit(solution)/shard_map/jit(cholesky)/cholesky | solution.py:21
  38.2 11.9 %cholesky.189 = f32[128,128]{1,0:T(8,128)S(1)} custom-call(f32[128,128]{1,0:T(8,128)S(1)} %convolution_subtract_fusion.6), custom_call_target="Cholesky" | custom-call | tf_op jit(solution)/shard_map/jit(cholesky)/cholesky | solution.py:21
  52.3 4.1 while.6
  56.4 19.7 %custom-call.20 = f32[2,128,128]{1,2,0:T(8,128)S(1)} custom-call(f32[2,128,128]{2,1,0:T(8,128)S(1)} %get-tuple-element.26), custom_call_target="InvertDiagBlocksLowerTriangular" | custom-call | tf_op jit(solution)/shard_map/jit(_solve_triangular)/triangular_solve | solution.py:22
  76.1 2.3 fusion.9
  78.3 3.0 convolution_subtract_fusion.2
  82.5 1.9 fusion
  84.5 11.7 %cholesky.206 = f32[128,128]{1,0:T(8,128)S(1)} custom-call(f32[128,128]{1,0:T(8,128)S(1)} %cholesky.273), custom_call_target="Cholesky" | custom-call | tf_op jit(solution)/shard_map/jit(cholesky)/cholesky | solution.py:21
  96.9 10.2 %custom-call.21 = f32[1,128,128]{1,2,0:T(8,128)S(1)} custom-call(f32[1,128,128]{2,1,0:T(8,128)S(1)} %get-tuple-element.67), custom_call_target="InvertDiagBlocksLowerTriangular" | custom-call | tf_op jit(solution)/shard_map/jit(cholesky)/cholesky | solution.py:21
  107.6 11.7 %cholesky.223 = f32[128,128]{1,0:T(8,128)S(1)} custom-call(f32[128,128]{1,0:T(8,128)S(1)} %convolution_subtract_fusion.5), custom_call_target="Cholesky" | custom-call | tf_op jit(solution)/shard_map/jit(cholesky)/cholesky | solution.py:21
  123.3 4.0 while.7
  128.0 19.8 %custom-call.22 = f32[2,128,128]{1,2,0:T(8,128)S(1)} custom-call(f32[2,128,128]{2,1,0:T(8,128)S(1)} %get-tuple-element.27), custom_call_target="InvertDiagBlocksLowerTriangular" | custom-call | tf_op jit(solution)/shard_map/jit(_solve_triangular)/triangular_solve | solution.py:22
  148.9 1.9 convolution_subtract_fusion.1
  151.9 26.7 %all-reduce.5.cloned.1.call-done = f32[256,256]{0,1:T(8,128)} async-done(((f32[256,256]{0,1:T(8,128)}), f32[256,256]{0,1:T(8,128)}) %all-reduce.5.cloned.1.call-update) | async-done | bytes 262160 | tf_op jit(solution)/shard_map/psum | solution.py:38
  180.7 11.7 %cholesky.240 = f32[128,128]{1,0:T(8,128)S(1)} custom-call(f32[128,128]{1,0:T(8,128)S(1)} %cholesky.276), custom_call_target="Cholesky" | custom-call | tf_op jit(solution)/shard_map/jit(cholesky)/cholesky | solution.py:39
  193.1 9.8 %custom-call.23 = f32[1,128,128]{1,2,0:T(8,128)S(1)} custom-call(f32[1,128,128]{2,1,0:T(8,128)S(1)} %get-tuple-element.63), custom_call_target="InvertDiagBlocksLowerTriangular" | custom-call | tf_op jit(solution)/shard_map/jit(cholesky)/cholesky | solution.py:39
  203.4 11.9 %cholesky.257 = f32[128,128]{1,0:T(8,128)S(1)} custom-call(f32[128,128]{1,0:T(8,128)S(1)} %convolution_subtract_fusion.4), custom_call_target="Cholesky" | custom-call | tf_op jit(solution)/shard_map/jit(cholesky)/cholesky | solution.py:39
  217.5 4.1 while.5
  221.6 19.7 %custom-call.15 = f32[2,128,128]{1,2,0:T(8,128)S(1)} custom-call(f32[2,128,128]{2,1,0:T(8,128)S(1)} %get-tuple-element.19), custom_call_target="InvertDiagBlocksLowerTriangular" | custom-call | tf_op jit(solution)/shard_map/jit(_solve_triangular)/triangular_solve | solution.py:40
  242.3 4.8 convolution_select_fusion
  247.1 84.5 %all-reduce.7.cloned.1.call-done = f32[2048,256]{1,0:T(8,128)} async-done(((f32[2048,256]{1,0:T(8,128)}), f32[2048,256]{1,0:T(8,128)}) %all-reduce.7.cloned.1.call-update) | async-done | bytes 2097168 | tf_op jit(solution)/shard_map/psum | solution.py:12
  331.7 18.6 %fusion.58 = f32[256,2048]{1,0:T(8,128)} fusion(f32[2048,256]{1,0:T(8,128)} %all-reduce.7.cloned.1.call-done, f32[2048,2048]{1,0:T(8,128)} %param.4), kind=kOutput, calls=%fused_computation.107 | convolution fusion | flops 12884901888 | bytes 20971520 | tf_op jit(solution)/shard_map/dot_general | solution.py:16
  350.3 17.9 %copy.7 = f32[2048,2048]{0,1:T(8,128)} copy(f32[2048,2048]{1,0:T(8,128)} %param.4) | data formatting | bytes 33554432 | tf_op args[0]
  369.6 2.9 copy.8
  372.5 39.7 %all-reduce.9.cloned.1.call-done = f32[256,2048]{1,0:T(8,128)} async-done(((f32[256,2048]{1,0:T(8,128)}), f32[256,2048]{1,0:T(8,128)}) %all-reduce.9.cloned.1.call-update) | async-done | bytes 2097168 | tf_op jit(solution)/shard_map/psum | solution.py:43
  412.2 19.5 %convolution_subtract_fusion = f32[2048,2048]{0,1:T(8,128)} fusion(f32[2048,2048]{0,1:T(8,128)} %copy.7, f32[2048,256]{1,0:T(8,128)S(1)} %copy-done, f32[256,2048]{1,0:T(8,128)} %all-reduce.9.cloned.1.call-done), kind=kOutput, calls=%fused_computation.7 | convolution fusion | flops 12889096192 | bytes 37748736 | tf_op jit(solution)/shard_map/dot_general | solution.py:16
  431.7 13.3 %slice.80 = f32[2048,1792]{0,1:T(8,128)} slice(f32[2048,2048]{0,1:T(8,128)} %convolution_subtract_fusion), slice={[0:2048], [256:2048]} | slice | bytes 29360128 | tf_op jit(solution)/shard_map/slice | solution.py:49
  445.0 16.6 %maximum_select_fusion = f32[2048,2048]{0,1:T(8,128)} fusion(f32[2048,2048]{0,1:T(8,128)} %convolution_subtract_fusion, f32[2048,1792]{0,1:T(8,128)} %slice.80, f32[2048,256]{0,1:T(8,128)S(1)} %copy-done.1, pred[]{:T(512)S(6)} %eq.4), kind=kLoop, calls=%fused_computation.6 | loop fusion | flops 8388608 | bytes 50331648 | tf_op jit(solution)/shard_map/jit(_where)/select_n | solution.py:50
  461.5 17.6 %copy.9 = f32[2048,2048]{1,0:T(8,128)} copy(f32[2048,2048]{0,1:T(8,128)} %maximum_select_fusion) | data formatting | bytes 33554432
  (77 shorter events, 29.7 us)
Async XLA Ops:
  7.2 171.4 %all-reduce.5.cloned.1.call-start = ((), (), s32[]{:S(2)}) async-start(), calls=%async_computation | async-start | bytes 524288 | tf_op jit(solution)/shard_map/psum | solution.py:38
  123.2 208.5 %all-reduce.7.cloned.1.call-start = ((), (), s32[]{:S(2)}) async-start(), calls=%async_computation.1 | async-start | bytes 4194304 | tf_op jit(solution)/shard_map/psum | solution.py:12
  127.3 0.7 copy-start.2
  247.1 165.1 %all-reduce.9.cloned.1.call-start = ((), (), s32[]{:S(2)}) async-start(), calls=%async_computation.2 | async-start | bytes 4194304 | tf_op jit(solution)/shard_map/psum | solution.py:43
  350.3 17.9 %copy-start = (f32[2048,256]{1,0:T(8,128)S(1)}, f32[2048,256]{1,0:T(8,128)}, u32[]{:S(2)}) copy-start(f32[2048,256]{1,0:T(8,128)} %all-reduce.7.cloned.1.call-done) | copy-start | bytes 6291460
  431.7 13.3 %copy-start.1 = (f32[2048,256]{0,1:T(8,128)S(1)}, f32[2048,256]{0,1:T(8,128)}, u32[]{:S(2)}) copy-start(f32[2048,256]{0,1:T(8,128)} %copy.8) | copy-start | bytes 6291460
Sparse Core Ops, SparseCore 0:
  123.3 55.2 all-reduce.4
  247.2 84.4 all-reduce.6
  350.4 61.8 all-reduce.8
where the time goes:
time: 497 us; the launch traced here: 488 us
  other arithmetic  182 us (37%)
  waiting for transfers between devices  151 us (30%)
  local copies, waits for them, and re-layouts  70.6 us (14%)
  matrix products  64.9 us (13%)
  between operations  18.4 us (4%)
    psum x1, waiting for transfers between devices, broadcast(): return lax.psum(jnp.where(mine, shard, jnp.zeros_like(shard)), axis)  84.5 us
    another operation x13, other arithmetic, cholesky_pass(): lower = jnp.linalg.cholesky(gram)  69.2 us
    dot_general x7, matrix products, multiply(): jnp.dot(left, right, precision=precise, preferred_element_type=jnp.float32)  52.1 us
    psum x1, waiting for transfers between devices, shards(): full_upper = lax.psum(multiply(basis.T, matrix), 'row')  39.7 us
    another operation x5, other arithmetic, cholesky_pass(): basis = jax.scipy.linalg.solve_triangular(lower, block.T, lower=True).T  39.6 us
    unnamed x8, local copies, waits for them, and re-layouts  36.2 us
    another operation x7, other arithmetic, shards(): whole_upper = jnp.linalg.cholesky(total_gram).T  34.9 us
    psum x1, waiting for transfers between devices, shards(): total_gram = lax.psum(multiply(local_upper.T, local_upper), 'row')  26.7 us
  transfers between devices with their start and end apart: 3, of which 3 were waited for; matrix products, arithmetic and copies ran while one was open for 10% of the time, Pallas kernels for 0%

commit v1 on v0

--- a/solution.py
+++ b/solution.py
@@ -7,9 +7,13 @@
 precise = lax.Precision.HIGHEST
 
 
+def sites_settle(sample, chip_axis):
+    return jnp.sum(lax.all_gather(sample, chip_axis), axis=0)
+
+
 def broadcast(shard, axis, root):
     mine = lax.axis_index(axis) == root
-    return lax.psum(jnp.where(mine, shard, jnp.zeros_like(shard)), axis)
+    return sites_settle(jnp.where(mine, shard, jnp.zeros_like(shard)), axis)
 
 
 def multiply(left, right):

time: 497 us -> 564 us (1.13)
  waiting for transfers between devices: 151 us -> 213 us
  other arithmetic: 182 us -> 188 us
    all_gather x0 -> x1, waiting for transfers between devices: none -> 146 us  [sites_settle(): return jnp.sum(lax.all_gather(sample, chip_axis), axis=0)]
    psum x1 -> x0, waiting for transfers between devices: 84.5 us -> none  [broadcast(): return lax.psum(jnp.where(mine, shard, jnp.zeros_like(shard)), axis)]
    unnamed x8 -> x6, local copies, waits for them, and re-layouts: 36.2 us -> 36.1 us
  transfers between devices with their start and end apart: 3 -> 3, of which waited for: 3 -> 3; matrix products, arithmetic and copies ran while one was open for 10% -> 9% of each run, Pallas kernels for 0% -> 0%
where the time goes in v1:
time: 564 us; the launch traced here: 554 us
  waiting for transfers between devices  213 us (38%)
  other arithmetic  188 us (33%)
  local copies, waits for them, and re-layouts  69.4 us (12%)
  matrix products  64.3 us (11%)
  between operations  18.4 us (3%)
    all_gather x1, waiting for transfers between devices, sites_settle(): return jnp.sum(lax.all_gather(sample, chip_axis), axis=0)  146 us
    another operation x13, other arithmetic, cholesky_pass(): lower = jnp.linalg.cholesky(gram)  69.2 us
    dot_general x7, matrix products, multiply(): jnp.dot(left, right, precision=precise, preferred_element_type=jnp.float32)  51.6 us
    psum x1, waiting for transfers between devices, shards(): full_upper = lax.psum(multiply(basis.T, matrix), 'row')  40.3 us
    another operation x5, other arithmetic, cholesky_pass(): basis = jax.scipy.linalg.solve_triangular(lower, block.T, lower=True).T  39.6 us
    unnamed x6, local copies, waits for them, and re-layouts  36.1 us
    another operation x7, other arithmetic, shards(): whole_upper = jnp.linalg.cholesky(total_gram).T  34.9 us
    psum x1, waiting for transfers between devices, shards(): total_gram = lax.psum(multiply(local_upper.T, local_upper), 'row')  26.7 us
  transfers between devices with their start and end apart: 3, of which 3 were waited for; matrix products, arithmetic and copies ran while one was open for 9% of the time, Pallas kernels for 0%

profile of v1, /device:TPU:8, one launch (start us, length us, event | category | flops | bytes accessed | tf_op | source)
XLA Modules:
  0.0 554.0 jit_solution(8036102069344924277)
XLA Ops:
  7.2 5.7 %fusion.7 = f32[256,256]{1,0:T(8,128)S(1)} fusion(f32[2048,2048]{1,0:T(8,128)} %param.4), kind=kOutput, calls=%fused_computation.19 | convolution fusion | flops 1610612736 | bytes 2359296 | tf_op jit(solution)/shard_map/dot_general | solution.py:20
  12.9 3.0 slice_bitcast_fusion
  16.2 11.7 %cholesky.172 = f32[128,128]{1,0:T(8,128)S(1)} custom-call(f32[128,128]{1,0:T(8,128)S(1)} %cholesky.270), custom_call_target="Cholesky" | custom-call | tf_op jit(solution)/shard_map/jit(cholesky)/cholesky | solution.py:25
  27.9 9.8 %custom-call.19 = f32[1,128,128]{1,2,0:T(8,128)S(1)} custom-call(f32[1,128,128]{2,1,0:T(8,128)S(1)} %get-tuple-element.73), custom_call_target="InvertDiagBlocksLowerTriangular" | custom-call | tf_op jit(solution)/shard_map/jit(cholesky)/cholesky | solution.py:25
  38.2 11.9 %cholesky.189 = f32[128,128]{1,0:T(8,128)S(1)} custom-call(f32[128,128]{1,0:T(8,128)S(1)} %convolution_subtract_fusion.6), custom_call_target="Cholesky" | custom-call | tf_op jit(solution)/shard_map/jit(cholesky)/cholesky | solution.py:25
  52.3 4.1 while.6
  56.4 19.7 %custom-call.20 = f32[2,128,128]{1,2,0:T(8,128)S(1)} custom-call(f32[2,128,128]{2,1,0:T(8,128)S(1)} %get-tuple-element.26), custom_call_target="InvertDiagBlocksLowerTriangular" | custom-call | tf_op jit(solution)/shard_map/jit(_solve_triangular)/triangular_solve | solution.py:26
  76.1 2.3 fusion.9
  78.3 3.0 convolution_subtract_fusion.2
  82.5 1.9 fusion
  84.5 11.7 %cholesky.206 = f32[128,128]{1,0:T(8,128)S(1)} custom-call(f32[128,128]{1,0:T(8,128)S(1)} %cholesky.273), custom_call_target="Cholesky" | custom-call | tf_op jit(solution)/shard_map/jit(cholesky)/cholesky | solution.py:25
  96.9 10.2 %custom-call.21 = f32[1,128,128]{1,2,0:T(8,128)S(1)} custom-call(f32[1,128,128]{2,1,0:T(8,128)S(1)} %get-tuple-element.69), custom_call_target="InvertDiagBlocksLowerTriangular" | custom-call | tf_op jit(solution)/shard_map/jit(cholesky)/cholesky | solution.py:25
  107.6 11.7 %cholesky.223 = f32[128,128]{1,0:T(8,128)S(1)} custom-call(f32[128,128]{1,0:T(8,128)S(1)} %convolution_subtract_fusion.5), custom_call_target="Cholesky" | custom-call | tf_op jit(solution)/shard_map/jit(cholesky)/cholesky | solution.py:25
  123.3 4.0 while.7
  128.0 19.8 %custom-call.22 = f32[2,128,128]{1,2,0:T(8,128)S(1)} custom-call(f32[2,128,128]{2,1,0:T(8,128)S(1)} %get-tuple-element.27), custom_call_target="InvertDiagBlocksLowerTriangular" | custom-call | tf_op jit(solution)/shard_map/jit(_solve_triangular)/triangular_solve | solution.py:26
  151.9 26.7 %all-reduce.4.cloned.1.call-done = f32[256,256]{0,1:T(8,128)} async-done(((f32[256,256]{0,1:T(8,128)}), f32[256,256]{0,1:T(8,128)}) %all-reduce.4.cloned.1.call-update) | async-done | bytes 262160 | tf_op jit(solution)/shard_map/psum | solution.py:42
  180.7 11.7 %cholesky.240 = f32[128,128]{1,0:T(8,128)S(1)} custom-call(f32[128,128]{1,0:T(8,128)S(1)} %cholesky.276), custom_call_target="Cholesky" | custom-call | tf_op jit(solution)/shard_map/jit(cholesky)/cholesky | solution.py:43
  193.1 9.8 %custom-call.23 = f32[1,128,128]{1,2,0:T(8,128)S(1)} custom-call(f32[1,128,128]{2,1,0:T(8,128)S(1)} %get-tuple-element.65), custom_call_target="InvertDiagBlocksLowerTriangular" | custom-call | tf_op jit(solution)/shard_map/jit(cholesky)/cholesky | solution.py:43
  203.4 11.9 %cholesky.257 = f32[128,128]{1,0:T(8,128)S(1)} custom-call(f32[128,128]{1,0:T(8,128)S(1)} %convolution_subtract_fusion.4), custom_call_target="Cholesky" | custom-call | tf_op jit(solution)/shard_map/jit(cholesky)/cholesky | solution.py:43
  217.5 4.1 while.5
  221.6 19.7 %custom-call.15 = f32[2,128,128]{1,2,0:T(8,128)S(1)} custom-call(f32[2,128,128]{2,1,0:T(8,128)S(1)} %get-tuple-element.19), custom_call_target="InvertDiagBlocksLowerTriangular" | custom-call | tf_op jit(solution)/shard_map/jit(_solve_triangular)/triangular_solve | solution.py:44
  242.3 4.8 convolution_select_fusion
  247.1 146.2 %all-gather.3.cloned.1.call-done = f32[8192,256]{1,0:T(8,128)} async-done(((f32[2048,256]{1,0:T(8,128)}), f32[8192,256]{1,0:T(8,128)}) %all-gather.3.cloned.1.call-update) | async-done | bytes 8388624 | tf_op jit(solution)/shard_map/all_gather | solution.py:11
  393.3 4.2 reduce_sum.9
  397.5 18.0 %fusion.58 = f32[256,2048]{1,0:T(8,128)} fusion(f32[2048,256]{1,0:T(8,128)S(1)} %reduce_sum.9, f32[2048,2048]{1,0:T(8,128)} %param.4), kind=kOutput, calls=%fused_computation.107 | convolution fusion | flops 12884901888 | bytes 20971520 | tf_op jit(solution)/shard_map/dot_general | solution.py:20
  415.5 17.8 %copy.14 = f32[2048,2048]{0,1:T(8,128)} copy(f32[2048,2048]{1,0:T(8,128)} %param.4) | data formatting | bytes 33554432 | tf_op args[0]
  435.1 3.1 broadcast_multiply_fusion
  438.2 40.3 %all-reduce.6.cloned.1.call-done = f32[256,2048]{1,0:T(8,128)} async-done(((f32[256,2048]{1,0:T(8,128)}), f32[256,2048]{1,0:T(8,128)}) %all-reduce.6.cloned.1.call-update) | async-done | bytes 2097168 | tf_op jit(solution)/shard_map/psum | solution.py:47
  478.5 19.4 %convolution_subtract_fusion = f32[2048,2048]{0,1:T(8,128)} fusion(f32[2048,2048]{0,1:T(8,128)} %copy.14, f32[2048,256]{1,0:T(8,128)S(1)} %reduce_sum.9, f32[256,2048]{1,0:T(8,128)} %all-reduce.6.cloned.1.call-done), kind=kOutput, calls=%fused_computation.7 | convolution fusion | flops 12889096192 | bytes 37748736 | tf_op jit(solution)/shard_map/dot_general | solution.py:20
  498.0 13.3 %slice.80 = f32[2048,1792]{0,1:T(8,128)} slice(f32[2048,2048]{0,1:T(8,128)} %convolution_subtract_fusion), slice={[0:2048], [256:2048]} | slice | bytes 29360128 | tf_op jit(solution)/shard_map/slice | solution.py:53
  511.2 16.6 %maximum_select_fusion = f32[2048,2048]{0,1:T(8,128)} fusion(f32[2048,2048]{0,1:T(8,128)} %convolution_subtract_fusion, f32[2048,1792]{0,1:T(8,128)} %slice.80, f32[2048,256]{0,1:T(8,128)S(1)} %copy-done, pred[]{:T(512)S(6)} %eq.4), kind=kLoop, calls=%fused_computation.6 | loop fusion | flops 8388608 | bytes 50331648 | tf_op jit(solution)/shard_map/jit(_where)/select_n | solution.py:54
  527.8 17.6 %copy.15 = f32[2048,2048]{1,0:T(8,128)} copy(f32[2048,2048]{0,1:T(8,128)} %maximum_select_fusion) | data formatting | bytes 33554432
  (76 shorter events, 31.9 us)
Async XLA Ops:
  7.2 171.4 %all-reduce.4.cloned.1.call-start = ((), (), s32[]{:S(2)}) async-start(), calls=%async_computation | async-start | bytes 524288 | tf_op jit(solution)/shard_map/psum | solution.py:42
  123.2 270.1 %all-gather.3.cloned.1.call-start = ((), (), s32[]{:S(2)}) async-start(), calls=%async_computation.2 | async-start | bytes 10485760 | tf_op jit(solution)/shard_map/all_gather | solution.py:11
  127.3 0.7 copy-start.1
  247.1 231.4 %all-reduce.6.cloned.1.call-start = ((), (), s32[]{:S(2)}) async-start(), calls=%async_computation.1 | async-start | bytes 4194304 | tf_op jit(solution)/shard_map/psum | solution.py:47
  497.9 13.3 %copy-start = (f32[2048,256]{0,1:T(8,128)S(1)}, f32[2048,256]{0,1:T(8,128)}, u32[]{:S(2)}) copy-start(f32[2048,256]{0,1:T(8,128)} %broadcast_multiply_fusion) | copy-start | bytes 6291460
Sparse Core Ops, SparseCore 0:
  123.3 55.2 all-reduce.3
  247.2 146.0 all-gather.2
  415.6 62.8 all-reduce.5
